TPU v7x, 16 devices: a whole 2x2x2 slice. The times are simulated.
16 devices in a mesh: dp: 4 (over z, y), tp: 4 (over x, core).
Axes of the slice: x: 2, y: 2, z: 2, core: 2. Of those that a mesh axis runs over, the one named last changes fastest.
Arguments:
- x: bfloat16 [512, 2048], P('dp'), parts along dimension 0
- g_attn: bfloat16 [2, 2048], replicated
- w_qkv: bfloat16 [2, 2048, 3072], P(None, None, 'tp')
- w_o: bfloat16 [2, 2048, 2048], P(None, 'tp')
- g_mlp: bfloat16 [2, 2048], replicated
- w_gate: bfloat16 [2, 2048, 8192], P(None, None, 'tp')
- w_up: bfloat16 [2, 2048, 8192], P(None, None, 'tp')
- w_down: bfloat16 [2, 8192, 2048], P(None, 'tp')
- k_cache: bfloat16 [2, 512, 512, 8, 64], P(None, 'dp', None, 'tp'), parts along dimension 1
- v_cache: bfloat16 [2, 512, 512, 8, 64], P(None, 'dp', None, 'tp'), parts along dimension 1
- lengths: int32 [512], P('dp'), parts along dimension 0
Outputs:
- output: bfloat16 [512, 2048], P('dp'), parts along dimension 0
There are 4 independent parts. A program takes and returns all parts, laid end to end along the dimension named above; an argument that names none is the same for every part.
All inputs are finite; a program needn't handle non-finite values.
Results may differ from a plain program's by a relative error of at most 0.018017.
Values are sent between devices in bfloat16 or wider.
A program may use at most 1 GiB of HBM per device.

v0:
```python
import jax
import jax.numpy as jnp
from jax import lax
from jax.sharding import PartitionSpec as P

EPS = 1e-5
ROPE_THETA = 500000.0


def _rmsnorm(x, g):
    xf = x.astype(jnp.float32)
    r = lax.rsqrt(jnp.mean(xf * xf, axis=-1, keepdims=True) + EPS)
    return (xf * r * g.astype(jnp.float32)).astype(jnp.bfloat16)


def _rope(t, pos):
    hd = t.shape[-1]
    half = hd // 2
    inv = ROPE_THETA ** (-jnp.arange(half, dtype=jnp.float32) * 2.0 / hd)
    ang = pos.astype(jnp.float32)[:, None] * inv[None, :]
    shape = (pos.shape[0],) + (1,) * (t.ndim - 2) + (half,)
    c = jnp.cos(ang).reshape(shape)
    s = jnp.sin(ang).reshape(shape)
    tf = t.astype(jnp.float32)
    t1, t2 = tf[..., :half], tf[..., half:]
    return jnp.concatenate([t1 * c - t2 * s, t2 * c + t1 * s], axis=-1).astype(jnp.bfloat16)


def _attention(q, k_new, v_new, kc, vc, lengths):
    scale = q.shape[-1] ** -0.5
    s_c = jnp.einsum('bjgd,bsjd->bjgs', q, kc, preferred_element_type=jnp.float32) * scale
    mask = jnp.arange(kc.shape[1])[None, :] < lengths[:, None]
    s_c = jnp.where(mask[:, None, None, :], s_c, -jnp.inf)
    s_n = jnp.einsum('bjgd,bjd->bjg', q, k_new, preferred_element_type=jnp.float32) * scale
    m = jnp.maximum(jnp.max(s_c, axis=-1), s_n)
    p_c = jnp.exp(s_c - m[..., None])
    p_n = jnp.exp(s_n - m)
    den = jnp.sum(p_c, axis=-1) + p_n
    o = jnp.einsum('bjgs,bsjd->bjgd', p_c.astype(jnp.bfloat16), vc, preferred_element_type=jnp.float32)
    o = o + p_n[..., None] * v_new.astype(jnp.float32)[:, :, None, :]
    return o / den[..., None]


def solution(mesh):
    def body(x, g_attn, w_qkv, w_o, g_mlp, w_gate, w_up, w_down, k_cache, v_cache, lengths):
        n = x.shape[0]
        kvl, hd = k_cache.shape[3], k_cache.shape[4]
        grp = w_o.shape[1] // hd // kvl
        for l in range(w_qkv.shape[0]):
            a = _rmsnorm(x, g_attn[l])
            qkv = jnp.dot(a, w_qkv[l], preferred_element_type=jnp.float32).astype(jnp.bfloat16)
            qkv = qkv.reshape(n, kvl, grp + 2, hd)
            q = _rope(qkv[:, :, :grp], lengths)
            k = _rope(qkv[:, :, grp], lengths)
            att = _attention(q, k, qkv[:, :, grp + 1], k_cache[l], v_cache[l], lengths)
            att = att.astype(jnp.bfloat16).reshape(n, kvl * grp * hd)
            o = jnp.dot(att, w_o[l], preferred_element_type=jnp.float32).astype(jnp.bfloat16)
            h = (x.astype(jnp.float32) + lax.psum(o, 'tp').astype(jnp.float32)).astype(jnp.bfloat16)
            b = _rmsnorm(h, g_mlp[l])
            gate = jnp.dot(b, w_gate[l], preferred_element_type=jnp.float32)
            up = jnp.dot(b, w_up[l], preferred_element_type=jnp.float32)
            act = (jax.nn.silu(gate) * up).astype(jnp.bfloat16)
            m = jnp.dot(act, w_down[l], preferred_element_type=jnp.float32).astype(jnp.bfloat16)
            x = (h.astype(jnp.float32) + lax.psum(m, 'tp').astype(jnp.float32)).astype(jnp.bfloat16)
        return x

    col = P(None, None, 'tp')
    row = P(None, 'tp', None)
    cache = P(None, 'dp', None, 'tp', None)
    return jax.shard_map(body, mesh=mesh,
                         in_specs=(P('dp', None), P(), col, row, P(), col, col, row, cache, cache, P('dp')),
                         out_specs=P('dp', None), check_vma=False)
```

profile of v0, /device:TPU:0, one launch (start us, length us, event | category | flops | bytes accessed | tf_op | source)
XLA Modules:
  0.0 225.4 jit_solution(202831096857378481)
XLA Ops:
  8.0 1.2 fusion.78
  9.2 0.8 slice_convert_fusion.3
  10.0 2.7 %fusion.66 = bf16[128,768]{1,0:T(8,128)(2,1)S(1)} fusion(bf16[2,2048,768]{2,1,0:T(8,128)(2,1)} %param.13, bf16[128,2048]{1,0:T(8,128)(2,1)} %param.11, f32[2048]{0:T(1024)S(1)} %bitcast.139, f32[128]{0:T(128)S(1)} %add_rsqrt_fusion.3), kind=kOutput, calls=%fused_computation.68 | convolution fusion | flops 403800064 | bytes 3875328 | tf_op jit(solution)/shard_map/dot_general | solution.py:51
  15.1 8.3 %fusion.58 = (f32[128,2,4]{2,1,0:T(2,128)S(1)}, f32[128,2,4,512]{3,2,1,0:T(4,128)S(1)}) fusion(pred[128,512]{1,0:T(8,128)(4,1)S(1)} %iota_compare_fusion, bf16[128,2,4,64]{3,2,1,0:T(4,128)(2,1)S(1)} %pad_maximum_fusion, bf16[2,128,512,2,64]{2,4,3,1,0:T(8,128)(2,1)} %param.19), kind=kOutput, calls=%fused_computation.52 | convolution fusion | flops 68680704 | bytes 19075072 | tf_op jit(solution)/shard_map/bjgd,bsjd->bjgs/dot_general | solution.py:31
  23.5 1.7 fusion.72
  25.4 8.3 %fusion.117 = bf16[128,2,4,64]{3,2,1,0:T(4,128)(2,1)S(1)} fusion(bf16[2,128,512,2,64]{2,4,3,1,0:T(8,128)(2,1)} %param.20, f32[128,2,4,512]{3,2,1,0:T(4,128)S(1)} %get-tuple-element.32, f32[128,2,4]{2,1,0:T(2,128)S(1)} %multiply_maximum_fusion.1, pred[128,512]{1,0:T(8,128)(4,1)S(1)} %iota_compare_fusion, f32[128,2,4]{2,1,0:T(2,128)S(1)} %get-tuple-element.11, ...), kind=kOutput, calls=%fused_computation.101 | convolution fusion | flops 69468160 | bytes 19148800 | tf_op jit(solution)/shard_map/bjgs,bsjd->bjgd/dot_general | solution.py:39
  33.9 2.9 %convolution_convert_fusion.1 = bf16[128,2048]{1,0:T(8,128)(2,1)} fusion(bf16[128,512]{0,1:T(8,128)(2,1)S(1)} %bitcast.132, bf16[2,512,2048]{2,1,0:T(8,128)(2,1)} %param.14), kind=kOutput, calls=%fused_computation.43 | convolution fusion | flops 268697600 | bytes 2752512 | tf_op jit(solution)/shard_map/dot_general | solution.py:57
  37.1 32.3 %all-reduce.5.cloned.1.call-done = bf16[128,2048]{1,0:T(8,128)(2,1)} async-done(((bf16[128,2048]{1,0:T(8,128)(2,1)}), bf16[128,2048]{1,0:T(8,128)(2,1)}) %all-reduce.5.cloned.1.call-update) | async-done | bytes 524304 | tf_op jit(solution)/shard_map/psum | solution.py:58
  69.4 1.3 fusion.82
  70.7 4.7 %fusion.22 = f32[128,2048]{1,0:T(8,128)S(1)} fusion(bf16[2,2048,2048]{2,1,0:T(8,128)(2,1)} %param.16, bf16[128,2048]{1,0:T(8,128)(2,1)S(1)} %get-tuple-element.10, f32[2048]{0:T(1024)S(1)} %bitcast.137, f32[128]{0:T(128)S(1)} %add_rsqrt_fusion.2), kind=kOutput, calls=%fused_computation.22 | convolution fusion | flops 1074790400 | bytes 9970176 | tf_op jit(solution)/shard_map/dot_general | solution.py:60
  75.4 9.2 %fusion.42 = bf16[128,2048]{1,0:T(8,128)(2,1)} fusion(bf16[2,2048,2048]{2,1,0:T(8,128)(2,1)} %param.18, bf16[2,2048,2048]{2,1,0:T(8,128)(2,1)} %param.17, f32[128,2048]{1,0:T(8,128)S(1)} %fusion.22, bf16[128,2048]{1,0:T(8,128)(2,1)S(1)} %get-tuple-element.10, f32[2048]{0:T(1024)S(1)} %bitcast.138, f32[128]{0:T(128)S(1)} %add_rsqrt_fusion.2), kind=kOutput, calls=%fused_computation.38 | convolution fusion | flops 2150367232 | bytes 18883072 | tf_op jit(solution)/shard_map/dot_general | solution.py:63
  84.7 29.7 %all-reduce.7.cloned.1.call-done = bf16[128,2048]{1,0:T(8,128)(2,1)} async-done(((bf16[128,2048]{1,0:T(8,128)(2,1)}), bf16[128,2048]{1,0:T(8,128)(2,1)}) %all-reduce.7.cloned.1.call-update) | async-done | bytes 524304 | tf_op jit(solution)/shard_map/psum | solution.py:64
  114.3 1.3 fusion.86
  115.7 2.7 %fusion.69 = bf16[128,768]{1,0:T(8,128)(2,1)S(1)} fusion(bf16[2,2048,768]{2,1,0:T(8,128)(2,1)} %param.13, f32[2048]{0:T(1024)S(1)} %bitcast.136, f32[128]{0:T(128)S(1)} %add_rsqrt_fusion.1, bf16[128,2048]{1,0:T(8,128)(2,1)S(1)} %get-tuple-element.10, bf16[128,2048]{1,0:T(8,128)(2,1)} %all-reduce.7.cloned.1.call-done), kind=kOutput, calls=%fused_computation.69 | convolution fusion | flops 404848640 | bytes 4399616 | tf_op jit(solution)/shard_map/dot_general | solution.py:51
  120.0 8.3 %fusion.59 = (f32[128,2,4]{2,1,0:T(2,128)S(1)}, f32[128,2,4,512]{3,2,1,0:T(4,128)S(1)}) fusion(pred[128,512]{1,0:T(8,128)(4,1)S(1)} %iota_compare_fusion, bf16[128,2,4,64]{3,2,1,0:T(4,128)(2,1)S(1)} %pad_maximum_fusion.1, bf16[2,128,512,2,64]{2,4,3,1,0:T(8,128)(2,1)} %param.19), kind=kOutput, calls=%fused_computation.53 | convolution fusion | flops 68680704 | bytes 19075072 | tf_op jit(solution)/shard_map/bjgd,bsjd->bjgs/dot_general | solution.py:31
  128.8 1.7 fusion.74
  130.7 8.3 %fusion.107 = bf16[128,2,4,64]{3,2,1,0:T(4,128)(2,1)S(1)} fusion(bf16[2,128,512,2,64]{2,4,3,1,0:T(8,128)(2,1)} %param.20, f32[128,2,4,512]{3,2,1,0:T(4,128)S(1)} %get-tuple-element.34, f32[128,2,4]{2,1,0:T(2,128)S(1)} %multiply_maximum_fusion, pred[128,512]{1,0:T(8,128)(4,1)S(1)} %iota_compare_fusion, f32[128,2,4]{2,1,0:T(2,128)S(1)} %get-tuple-element.7, ...), kind=kOutput, calls=%fused_computation.99 | convolution fusion | flops 69468160 | bytes 19148800 | tf_op jit(solution)/shard_map/bjgs,bsjd->bjgd/dot_general | solution.py:39
  139.2 2.9 %convolution_convert_fusion = bf16[128,2048]{1,0:T(8,128)(2,1)} fusion(bf16[128,512]{0,1:T(8,128)(2,1)S(1)} %bitcast.133, bf16[2,512,2048]{2,1,0:T(8,128)(2,1)} %param.14), kind=kOutput, calls=%fused_computation.42 | convolution fusion | flops 268697600 | bytes 2752512 | tf_op jit(solution)/shard_map/dot_general | solution.py:57
  142.4 29.4 %all-reduce.9.cloned.1.call-done = bf16[128,2048]{1,0:T(8,128)(2,1)} async-done(((bf16[128,2048]{1,0:T(8,128)(2,1)}), bf16[128,2048]{1,0:T(8,128)(2,1)}) %all-reduce.9.cloned.1.call-update) | async-done | bytes 524304 | tf_op jit(solution)/shard_map/psum | solution.py:58
  171.8 1.4 fusion.90
  173.2 4.7 %fusion.16 = f32[128,2048]{1,0:T(8,128)S(1)} fusion(bf16[2,2048,2048]{2,1,0:T(8,128)(2,1)} %param.16, bf16[128,2048]{1,0:T(8,128)(2,1)S(1)} %get-tuple-element.6, f32[2048]{0:T(1024)S(1)} %bitcast.134, f32[128]{0:T(128)S(1)} %add_rsqrt_fusion), kind=kOutput, calls=%fused_computation.16 | convolution fusion | flops 1074790400 | bytes 9970176 | tf_op jit(solution)/shard_map/dot_general | solution.py:60
  177.9 9.2 %fusion.45 = bf16[128,2048]{1,0:T(8,128)(2,1)} fusion(bf16[2,2048,2048]{2,1,0:T(8,128)(2,1)} %param.18, bf16[2,2048,2048]{2,1,0:T(8,128)(2,1)} %param.17, f32[128,2048]{1,0:T(8,128)S(1)} %fusion.16, bf16[128,2048]{1,0:T(8,128)(2,1)S(1)} %get-tuple-element.6, f32[2048]{0:T(1024)S(1)} %bitcast.135, f32[128]{0:T(128)S(1)} %add_rsqrt_fusion), kind=kOutput, calls=%fused_computation.39 | convolution fusion | flops 2150367232 | bytes 18883072 | tf_op jit(solution)/shard_map/dot_general | solution.py:63
  187.2 29.7 %all-reduce.11.cloned.1.call-done = bf16[128,2048]{1,0:T(8,128)(2,1)} async-done(((bf16[128,2048]{1,0:T(8,128)(2,1)}), bf16[128,2048]{1,0:T(8,128)(2,1)}) %all-reduce.11.cloned.1.call-update) | async-done | bytes 524304 | tf_op jit(solution)/shard_map/psum | solution.py:64
  216.9 2.0 fusion.93
  (55 shorter events, 7.2 us)
Async XLA Ops:
  6.5 62.8 %all-reduce.5.cloned.1.call-start = ((), (), s32[]{:S(2)}) async-start(), calls=%async_computation | async-start | bytes 1048576 | tf_op jit(solution)/shard_map/psum | solution.py:58
  25.4 11.6 %copy-start.2 = (bf16[2,2048]{1,0:T(2,128)(2,1)S(1)}, bf16[2,2048]{1,0:T(2,128)(2,1)}, u32[]{:S(2)}) copy-start(bf16[2,2048]{1,0:T(2,128)(2,1)} %param.15) | copy-start | bytes 24580
  25.4 43.9 %copy-start.1 = (bf16[128,2048]{1,0:T(8,128)(2,1)S(1)}, bf16[128,2048]{1,0:T(8,128)(2,1)}, u32[]{:S(2)}) copy-start(bf16[128,2048]{1,0:T(8,128)(2,1)} %param.11) | copy-start | bytes 1572868
  36.8 77.5 %all-reduce.7.cloned.1.call-start = ((), (), s32[]{:S(2)}) async-start(), calls=%async_computation.1 | async-start | bytes 1048576 | tf_op jit(solution)/shard_map/psum | solution.py:64
  84.6 87.2 %all-reduce.9.cloned.1.call-start = ((), (), s32[]{:S(2)}) async-start(), calls=%async_computation.2 | async-start | bytes 1048576 | tf_op jit(solution)/shard_map/psum | solution.py:58
  130.7 41.1 %copy-start = (bf16[128,2048]{1,0:T(8,128)(2,1)S(1)}, bf16[128,2048]{1,0:T(8,128)(2,1)}, u32[]{:S(2)}) copy-start(bf16[128,2048]{1,0:T(8,128)(2,1)} %all-reduce.7.cloned.1.call-done) | copy-start | bytes 1572868
  142.1 74.8 %all-reduce.11.cloned.1.call-start = ((), (), s32[]{:S(2)}) async-start(), calls=%async_computation.3 | async-start | bytes 1048576 | tf_op jit(solution)/shard_map/psum | solution.py:64
Sparse Core Ops, SparseCore 0:
  36.9 32.3 all-reduce.4
  84.8 29.5 all-reduce.6
  142.2 29.5 all-reduce.8
  187.3 29.5 all-reduce.10
where the time goes:
time: 226 us; the launch traced here: 225 us
  waiting for transfers between devices  121 us (54%)
  matrix products  73 us (32%)
  other arithmetic  15.4 us (7%)
  between operations  13.5 us (6%)
    psum x2, waiting for transfers between devices, body(): lax.psum(o, 'tp').astype(jnp.float32)  61.7 us
    psum x2, waiting for transfers between devices, body(): lax.psum(m, 'tp').astype(jnp.float32)  59.4 us
    dot_general x2, matrix products, body(): jnp.dot(act, w_down[l], preferred_element_type=jnp.float32)  18.5 us
    dot_general x2, matrix products, _attention(): jnp.einsum('bjgd,bsjd->bjgs', q, kc, preferred_element_type=jnp.float32)  16.6 us
    dot_general x2, matrix products, _attention(): jnp.einsum('bjgs,bsjd->bjgd', p_c.astype(jnp.bfloat16), vc, preferred_ele...  16.6 us
    dot_general x2, matrix products, body(): gate = jnp.dot(b, w_gate[l], preferred_element_type=jnp.float32)  9.37 us
    dot_general x2, matrix products, body(): jnp.dot(att, w_o[l], preferred_element_type=jnp.float32)  5.72 us
    dot_general x2, matrix products, body(): jnp.dot(a, w_qkv[l], preferred_element_type=jnp.float32)  5.41 us
  transfers between devices with their start and end apart: 4, of which 4 were waited for; matrix products, arithmetic and copies ran while one was open for 0% of the time, Pallas kernels for 0%

commit v1 on v0

v1 whole, which is shorter than its diff:
```python
import functools

import jax
import jax.numpy as jnp
import numpy as np
from jax import lax
from jax.experimental import pallas as pl
from jax.experimental.pallas import tpu as pltpu
from jax.sharding import PartitionSpec as P

EPS = 1e-5
ROPE_THETA = 500000.0
MESH = pl.DeviceIdType.MESH
F32, BF16 = jnp.float32, jnp.bfloat16

LAYERS, ROWS, D, SEQ, HD = 2, 128, 2048, 512, 64
QKVL, FFL, HEADS = 768, 2048, 8
CB, NCB = 256, 8
CHUNK, NCH = 8, 16
RING = 12
LEAD = (6, RING)
QR, NQ = 32, 4
SCALE = HD ** -0.5
NT = (((1,), (1,)), ((), ()))


def _dot(a, b):
    return jnp.dot(a, b, preferred_element_type=F32)


def _kernel(lens, lenv, inv, g_attn, g_mlp, x_hbm, wqkv_hbm, wo_hbm, wg_hbm, wu_hbm, wd_hbm, k_hbm, v_hbm,
            out_hbm,
            kbuf, vbuf, wqkv, wo, wg, wu, wd, xb, hb, an, act, to, tm, r1o, r1m, co, cm, r2o, r2m,
            qkvs, qs, os_, kn, vn, cs, sn, pbuf, stat,
            ksem, vsem, qsem, osem, gsem, usem, dsem, xsem, ysem,
            s1o, a1o, s2o, a2o, s3o, a3o, s1m, a1m, s2m, a2m, s3m, a3m):
    me = lax.axis_index("tp")
    core = lax.rem(me, 2)
    partner = me + 1 - 2 * core
    across = lax.rem(me + 2, 4)
    barrier = pltpu.get_barrier_semaphore()
    for dev in (partner, across):
        pl.semaphore_signal(barrier, inc=1, device_id={"tp": dev}, device_id_type=MESH)

    def slot_of(l, c):
        return lax.rem(l * NCH + c, RING)

    def kcopy(l, c):
        s = slot_of(l, c)
        return pltpu.make_async_copy(k_hbm.at[l, pl.ds(c * CHUNK, CHUNK)], kbuf.at[s], ksem.at[s])

    def vcopy(l, c):
        s = slot_of(l, c)
        return pltpu.make_async_copy(v_hbm.at[l, pl.ds(c * CHUNK, CHUNK)], vbuf.at[s], vsem.at[s])

    def qcopy(l, i):
        r = pl.ds(i * 512, 512)
        return pltpu.make_async_copy(wqkv_hbm.at[l, r], wqkv.at[r], qsem.at[i])

    def ocopy(l, i):
        r = pl.ds(i * 256, 256)
        return pltpu.make_async_copy(wo_hbm.at[l, r], wo.at[r], osem.at[i])

    def gcopy(l, i):
        return pltpu.make_async_copy(wg_hbm.at[l, :, pl.ds(i * 512, 512)], wg.at[i], gsem.at[i])

    def ucopy(l, i):
        return pltpu.make_async_copy(wu_hbm.at[l, :, pl.ds(i * 512, 512)], wu.at[i], usem.at[i])

    def dcopy(l, i):
        return pltpu.make_async_copy(wd_hbm.at[l, :, pl.ds(i * CB, CB)], wd.at[i], dsem.at[i])

    def xcopy(i):
        return pltpu.make_async_copy(x_hbm.at[:, pl.ds(i * CB, CB)], xb.at[i], xsem.at[i])

    def ycopy(i):
        return pltpu.make_async_copy(xb.at[i], out_hbm.at[:, pl.ds(i * CB, CB)], ysem.at[i])

    def remote(src, dst, send, recv, dev):
        return pltpu.make_async_remote_copy(src_ref=src, dst_ref=dst, send_sem=send, recv_sem=recv,
                                            device_id={"tp": dev}, device_id_type=MESH)

    for i in range(NCB):
        xcopy(i).start()
    for i in range(4):
        qcopy(0, i).start()
    for c in range(LEAD[0]):
        kcopy(0, c).start()
        vcopy(0, c).start()
        if c == 1:
            for i in range(2):
                ocopy(0, i).start()

    lane = lax.broadcasted_iota(jnp.int32, (ROWS, 128), 1)
    low = lane < 64
    first = lax.rem(lane, 64) < 32

    pos = jnp.transpose(jnp.broadcast_to(lenv[...].astype(F32), (ROWS, 128)))
    ang = pos * inv[...]
    cs[...] = jnp.cos(ang)
    sn[...] = jnp.where(first, -jnp.sin(ang), jnp.sin(ang))

    def norm_rows(src, r0, g_ref, l):
        rows = pl.ds(r0, QR)
        ss = jnp.zeros((QR, CB), F32)
        for kb in range(NCB):
            v = src[kb, rows, :].astype(F32)
            ss = ss + v * v
        r = lax.rsqrt(jnp.sum(ss, axis=-1, keepdims=True) * (1.0 / D) + EPS)
        for kb in range(NCB):
            v = src[kb, rows, :].astype(F32)
            g = g_ref[l:l + 1, kb * CB:(kb + 1) * CB].astype(F32)
            an[rows, kb * CB:(kb + 1) * CB] = (v * r * g).astype(BF16)

    def rope(t):
        other = jnp.where(first, pltpu.roll(t, 96, 1), pltpu.roll(t, 32, 1))
        return (t * cs[...] + other * sn[...]).astype(BF16).astype(F32)

    def project(l):
        for i in range(4):
            qcopy(l, i).wait()
        for nb in range(3):
            z = _dot(an[...], wqkv[:, nb * 256:(nb + 1) * 256]).astype(BF16).astype(F32)
            qkvs[2 * nb] = z[:, :128]
            qkvs[2 * nb + 1] = z[:, 128:]
        for j in range(2):
            for pr in range(2):
                t = rope(qkvs[3 * j + pr])
                swapped = pltpu.roll(t, 64, 1)
                h = 4 * j + 2 * pr
                if j == 0:
                    even, odd = jnp.where(low, t, 0.0), jnp.where(low, swapped, 0.0)
                else:
                    even, odd = jnp.where(low, 0.0, swapped), jnp.where(low, 0.0, t)
                qs[pl.ds(h, ROWS, stride=HEADS), :] = even
                qs[pl.ds(h + 1, ROWS, stride=HEADS), :] = odd
        k0, k1 = rope(qkvs[2]), rope(qkvs[5])
        kn[...] = jnp.where(low, k0, pltpu.roll(k1, 64, 1))
        vn[...] = jnp.where(low, pltpu.roll(qkvs[2], 64, 1), qkvs[5])

    pos_s = lax.broadcasted_iota(jnp.int32, (8, SEQ), 1)

    def scores(l, c):
        s_ = slot_of(l, c)
        par = lax.rem(c, 2)
        for t in range(CHUNK):
            b = c * CHUNK + t
            q = qs[pl.ds(b * 8, 8), :]
            new = jnp.sum(q * kn[pl.ds(b, 1), :], axis=-1, keepdims=True) * SCALE
            s = _dot(q.astype(BF16), kbuf[s_, t]) * SCALE
            s = jnp.where(pos_s < lens[b], s, -jnp.inf)
            m = jnp.maximum(jnp.max(s, axis=-1, keepdims=True), new)
            p = jnp.exp(s - m)
            pn = jnp.exp(new - m)
            den = jnp.sum(p, axis=-1, keepdims=True) + pn
            pbuf[par, t] = p
            stat[par, 0, t] = jnp.broadcast_to(pn, (8, 128))
            stat[par, 1, t] = jnp.broadcast_to(den, (8, 128))

    def values(l, c):
        s_ = slot_of(l, c)
        par = lax.rem(c, 2)
        for t in range(CHUNK):
            b = c * CHUNK + t
            p = pbuf[par, t].astype(BF16)
            o = lax.dot_general(p, vbuf[s_, t], NT, preferred_element_type=F32)
            o = o + stat[par, 0, t] * vn[pl.ds(b, 1), :]
            os_[pl.ds(b * 8, 8), :] = o / stat[par, 1, t]

    low_q = lax.broadcasted_iota(jnp.int32, (QR, 128), 1) < 64

    def remote1o(q):
        rows = pl.ds(q * QR, QR)
        blocks = pl.ds((1 - core) * 4, 4)
        return remote(to.at[blocks, rows], r1o.at[:, rows], s1o.at[q], a1o.at[q], partner)

    def remote2o(q):
        rows = pl.ds(q * QR, QR)
        return remote(co.at[:, rows], r2o.at[:, rows], s2o.at[q], a2o.at[q], across)

    def remote3o(q):
        rows = pl.ds(q * QR, QR)
        blocks = pl.ds(core * 4, 4)
        return remote(hb.at[blocks, rows], hb.at[blocks, rows], s3o.at[q], a3o.at[q], partner)

    def out_proj(q):
        rows = pl.ds(q * QR, QR)
        pairs = []
        for j in range(2):
            for pr in range(2):
                h = 4 * j + 2 * pr
                e = os_[pl.ds(q * (QR * 8) + h, QR, stride=HEADS), :]
                o = os_[pl.ds(q * (QR * 8) + h + 1, QR, stride=HEADS), :]
                if j == 0:
                    pairs.append(jnp.where(low_q, e, pltpu.roll(o, 64, 1)).astype(BF16))
                else:
                    pairs.append(jnp.where(low_q, pltpu.roll(e, 64, 1), o).astype(BF16))
        att = jnp.concatenate(pairs, axis=1)
        for nb in range(4):
            z = _dot(att, wo[:, nb * 512:(nb + 1) * 512]).astype(BF16)
            to[2 * nb, rows, :] = z[:, :CB]
            to[2 * nb + 1, rows, :] = z[:, CB:]
        remote1o(q).start()

    def chip_sum_o(q):
        rows = pl.ds(q * QR, QR)
        remote1o(q).wait_recv()
        for i in range(4):
            co[i, rows, :] = (to[core * 4 + i, rows, :].astype(F32) + r1o[i, rows, :].astype(F32)).astype(BF16)
        remote2o(q).start()

    def group_sum_o(q):
        rows = pl.ds(q * QR, QR)
        remote2o(q).wait_recv()
        for i in range(4):
            z = co[i, rows, :].astype(F32) + r2o[i, rows, :].astype(F32)
            hb[core * 4 + i, rows, :] = (xb[core * 4 + i, rows, :].astype(F32) + z).astype(BF16)
        remote3o(q).start()

    def finish_o(q, l):
        remote3o(q).wait_recv()
        norm_rows(hb, q * QR, g_mlp, l)

    def remote1m(i):
        return remote(tm.at[(1 - core) * 4 + i], r1m.at[i], s1m.at[i], a1m.at[i], partner)

    def remote2m(i):
        return remote(cm.at[i], r2m.at[i], s2m.at[i], a2m.at[i], across)

    def remote3m(i):
        return remote(xb.at[core * 4 + i], xb.at[core * 4 + i], s3m.at[i], a3m.at[i], partner)

    for i in range(NCB):
        xcopy(i).wait()

    for l in range(LAYERS):
        lead = LEAD[l]

        @pl.loop(0, NQ)
        def _(q):
            norm_rows(xb, pl.multiple_of(q * QR, QR), g_attn, l)

        project(l)
        if l == 0:
            pl.semaphore_wait(barrier, 2)

        def refill(i):
            @pl.when(i + lead < NCH)
            def _():
                kcopy(l, i + lead).start()

            @pl.when(jnp.logical_and(i >= 1, i - 1 + lead < NCH))
            def _():
                vcopy(l, i - 1 + lead).start()
            t = i + lead - NCH

            @pl.when(jnp.logical_and(t >= 0, t < 4))
            def _():
                gcopy(l, t).start()
                ucopy(l, t).start()

            @pl.when(jnp.logical_and(t >= 4, t < 8))
            def _():
                dcopy(l, t - 4).start()
                dcopy(l, t).start()

        kcopy(l, 0).wait()
        scores(l, 0)
        refill(0)

        @pl.loop(1, NCH)
        def _(i):
            vcopy(l, i - 1).wait()
            kcopy(l, i).wait()
            values(l, i - 1)
            scores(l, i)
            refill(i)
            ph = lax.rem(i, 4)

            @pl.when(ph == 0)
            def _():
                @pl.when(i == 4)
                def _():
                    for j in range(2):
                        ocopy(l, j).wait()
                out_proj(i // 4 - 1)

            @pl.when(jnp.logical_and(ph == 2, i >= 6))
            def _():
                chip_sum_o((i - 6) // 4)

            @pl.when(jnp.logical_and(ph == 3, i >= 11))
            def _():
                group_sum_o((i - 11) // 4)

        vcopy(l, NCH - 1).wait()
        values(l, NCH - 1)
        for t in range(lead, 8):
            dcopy(l, t - 4).start()
            dcopy(l, t).start()
        out_proj(3)
        group_sum_o(2)
        finish_o(0, l)
        finish_o(1, l)
        chip_sum_o(3)
        finish_o(2, l)
        group_sum_o(3)
        finish_o(3, l)
        for q in range(NQ):
            remote1o(q).wait_send()
            remote2o(q).wait_send()
            remote3o(q).wait_send()

        if l + 1 < LAYERS:
            for i in range(4):
                qcopy(l + 1, i).start()
            for i in range(2):
                ocopy(l + 1, i).start()
            for c in range(LEAD[l + 1]):
                kcopy(l + 1, c).start()
                vcopy(l + 1, c).start()

        @pl.loop(0, 4)
        def _(n):
            gcopy(l, n).wait()
            ucopy(l, n).wait()
            gate = _dot(an[...], wg[n])
            up = _dot(an[...], wu[n])
            act[:, pl.ds(pl.multiple_of(n * 512, 512), 512)] = (jax.nn.silu(gate) * up).astype(BF16)

        @pl.loop(0, 4)
        def _(i):
            theirs, mine = (1 - core) * 4 + i, core * 4 + i
            dcopy(l, theirs).wait()
            dcopy(l, mine).wait()
            tm[theirs] = _dot(act[...], wd[theirs]).astype(BF16)
            tm[mine] = _dot(act[...], wd[mine]).astype(BF16)
            remote1m(i).start()

        @pl.loop(0, 4)
        def _(i):
            remote1m(i).wait_recv()
            cm[i] = (tm[core * 4 + i].astype(F32) + r1m[i].astype(F32)).astype(BF16)
            remote2m(i).start()

        @pl.loop(0, 4)
        def _(i):
            remote2m(i).wait_recv()
            z = cm[i].astype(F32) + r2m[i].astype(F32)
            xb[core * 4 + i] = (hb[core * 4 + i].astype(F32) + z).astype(BF16)
            remote3m(i).start()
            if l + 1 == LAYERS:
                ycopy(core * 4 + i).start()

        @pl.loop(0, 4)
        def _(i):
            remote3m(i).wait_recv()
            if l + 1 == LAYERS:
                ycopy((1 - core) * 4 + i).start()

        for i in range(4):
            remote1m(i).wait_send()
            remote2m(i).wait_send()
            remote3m(i).wait_send()

    for i in range(NCB):
        ycopy(i).wait()


def solution(mesh):
    half = HD // 2
    freq = np.float32(ROPE_THETA) ** (-np.arange(half, dtype=np.float32) * np.float32(2.0) / np.float32(HD))
    freq = np.tile(freq.astype(np.float32), 4)[None, :]

    def body(x, g_attn, w_qkv, w_o, g_mlp, w_gate, w_up, w_down, k_cache, v_cache, lengths):
        kt = jnp.transpose(k_cache, (0, 1, 3, 4, 2)).reshape(LAYERS, ROWS, 2 * HD, SEQ)
        vt = jnp.transpose(v_cache, (0, 1, 3, 4, 2)).reshape(LAYERS, ROWS, 2 * HD, SEQ)
        vm, hbm, sm = (pl.BlockSpec(memory_space=s) for s in (pltpu.VMEM, pl.ANY, pltpu.SMEM))
        V, DMA = pltpu.VMEM, pltpu.SemaphoreType.DMA
        scratch = [
            V((RING, CHUNK, 2 * HD, SEQ), BF16), V((RING, CHUNK, 2 * HD, SEQ), BF16),
            V((D, QKVL), BF16), V((512, D), BF16), V((4, D, 512), BF16), V((4, D, 512), BF16), V((NCB, FFL, CB), BF16),
            V((NCB, ROWS, CB), BF16), V((NCB, ROWS, CB), BF16), V((ROWS, D), BF16), V((ROWS, FFL), BF16),
            V((NCB, ROWS, CB), BF16), V((NCB, ROWS, CB), BF16),
            V((4, ROWS, CB), BF16), V((4, ROWS, CB), BF16), V((4, ROWS, CB), BF16), V((4, ROWS, CB), BF16),
            V((4, ROWS, CB), BF16), V((4, ROWS, CB), BF16),
            V((6, ROWS, 128), F32), V((ROWS * HEADS, 128), F32), V((ROWS * HEADS, 128), F32),
            V((ROWS, 128), F32), V((ROWS, 128), F32), V((ROWS, 128), F32), V((ROWS, 128), F32),
            V((2, CHUNK, 8, SEQ), F32), V((2, 2, CHUNK, 8, 128), F32),
            DMA((RING,)), DMA((RING,)), DMA((4,)), DMA((2,)), DMA((4,)), DMA((4,)), DMA((NCB,)), DMA((NCB,)),
            DMA((NCB,)),
        ] + [DMA((4,)) for _ in range(12)]
        return pl.pallas_call(
            _kernel,
            out_shape=jax.ShapeDtypeStruct((ROWS, D), BF16),
            in_specs=[sm, vm, vm, vm, vm] + [hbm] * 8,
            out_specs=hbm,
            scratch_shapes=scratch,
            compiler_params=pltpu.CompilerParams(collective_id=0, has_side_effects=True,
                                                 vmem_limit_bytes=67043328),
            name="decoder",
        )(lengths, lengths.reshape(1, ROWS), jnp.asarray(freq), g_attn, g_mlp, x, w_qkv, w_o, w_gate, w_up, w_down,
          kt, vt)

    col = P(None, None, 'tp')
    row = P(None, 'tp', None)
    cache = P(None, 'dp', None, 'tp', None)
    return jax.shard_map(body, mesh=mesh,
                         in_specs=(P('dp', None), P(), col, row, P(), col, col, row, cache, cache, P('dp')),
                         out_specs=P('dp', None), check_vma=False)
```

time: 226 us -> 80.7 us (0.36)
  waiting for transfers between devices: 121 us -> 0 us
  Pallas kernels: 0 us -> 78.6 us
  matrix products: 73 us -> 0 us
  other arithmetic: 15.4 us -> 0 us
  between operations: 13.5 us -> 0.01 us
    psum x4 -> x0, waiting for transfers between devices: 121 us -> none  [the longest x2 61.7 us: body(): lax.psum(o, 'tp').astype(jnp.float32)]
    pallas_call x0 -> x1, Pallas kernels: none -> 78.6 us  [body(): pl.pallas_call(_kernel, out_shape=jax.ShapeDtypeStruct((ROWS, D), BF16),...]
    dot_general x14 -> x0, matrix products: 73 us -> none  [the longest x2 18.5 us: body(): jnp.dot(act, w_down[l], preferred_element_type=jnp.float32)]
    reduce_sum x6 -> x0, other arithmetic: 8.63 us -> none  [the longest x4 5.21 us: _rmsnorm(): r = lax.rsqrt(jnp.mean(xf * xf, axis=-1, keepdims=True) + EPS)]
    convert_element_type x4 -> x0, other arithmetic: 2.76 us -> none  [the longest x1 1.96 us: body(): (h.astype(jnp.float32) + lax.psum(m, 'tp').astype(jnp.float32)).astype(jn...]
  transfers between devices with their start and end apart: 4 -> 0, of which waited for: 4 -> 0; matrix products, arithmetic and copies ran while one was open for 0% -> 0% of each run, Pallas kernels for 0% -> 0%
where the time goes in v1:
time: 80.7 us; the launch traced here: 80.5 us
  Pallas kernels  78.6 us (97%)
  local copies, waits for them, and re-layouts  1.88 us (2%)
    pallas_call x1, Pallas kernels, body(): pl.pallas_call(_kernel, out_shape=jax.ShapeDtypeStruct((ROWS, D), BF16),...  78.6 us
    unnamed x1, local copies, waits for them, and re-layouts  1.88 us

profile of v1, /device:TPU:0, one launch (start us, length us, event | category | flops | bytes accessed | tf_op | source)
XLA Modules:
  0.0 80.5 jit_solution(9186804745304516512)
XLA Ops:
  0.0 78.6 %decoder.1 = bf16[128,2048]{1,0:T(8,128)(2,1)} custom-call(s32[128]{0:T(128)} %lens.1, s32[1,128]{1,0:T(1,128)} %bitcast.9, f32[1,128]{1,0:T(1,128)} %constant.2.clone.inv, bf16[2,2048]{1,0:T(2,128)(2,1)} %g_attn.1, bf16[2,2048]{1,0:T(2,128)(2,1)} %g_mlp.1, bf16[128,2048]{1,0:T(8,128)(2,1)} %x_hbm.1, bf16[2,2048,768]{2,1,0:T(8,128)(2,1)} %wqkv_hbm.1, ...), custom_call_target="tpu_custom_call" | custom-call | tf_op jit(solution)/shard_map/decoder/pallas_call | solution.py:393
  78.6 1.9 %copy.14 = bf16[128,2048]{1,0:T(8,128)(2,1)} copy(bf16[128,2048]{1,0:T(8,128)(2,1)} %decoder.1) | data formatting | bytes 1048576

commit v2 on v1

v2 whole, which is shorter than its diff:
```python
import functools

import jax
import jax.numpy as jnp
import numpy as np
from jax import lax
from jax.experimental import pallas as pl
from jax.experimental.pallas import tpu as pltpu
from jax.sharding import PartitionSpec as P

EPS = 1e-5
ROPE_THETA = 500000.0
MESH = pl.DeviceIdType.MESH
F32, BF16 = jnp.float32, jnp.bfloat16

LAYERS, ROWS, D, SEQ, HD = 2, 128, 2048, 512, 64
QKVL, FFL, HEADS = 768, 2048, 8
CB, NCB = 256, 8
CHUNK, NCH = 16, 8
RING = 6
LEAD = (3, RING)
GV = 4
QR, NQ = 32, 4
HR = 64
SCALE = HD ** -0.5
NT = (((1,), (1,)), ((), ()))


def _dot(a, b):
    return jnp.dot(a, b, preferred_element_type=F32)


def _kernel(lens, lenv, inv, g_attn, g_mlp, x_hbm, wqkv_hbm, wo_hbm, wg_hbm, wu_hbm, wd_hbm, k_hbm, v_hbm,
            out_hbm,
            kbuf, vbuf, wqkv, wo, wg, wu, wd, xb, hb, an, act, to, tm, r1o, r1m, co, cm, r2o, r2m,
            qkvs, qs, os_, kn, vn, cs, sn, pbuf, stat, accs,
            ksem, vsem, qsem, osem, gsem, usem, dsem, xsem, ysem,
            s1o, a1o, s2o, a2o, s3o, a3o, s1m, a1m, s2m, a2m, s3m, a3m):
    me = lax.axis_index("tp")
    core = lax.rem(me, 2)
    partner = me + 1 - 2 * core
    across = lax.rem(me + 2, 4)
    barrier = pltpu.get_barrier_semaphore()
    for dev in (partner, across):
        pl.semaphore_signal(barrier, inc=1, device_id={"tp": dev}, device_id_type=MESH)

    def slot_of(l, c):
        return lax.rem(l * NCH + c, RING)

    def kcopy(l, c):
        s = slot_of(l, c)
        return pltpu.make_async_copy(k_hbm.at[l, pl.ds(c * CHUNK, CHUNK)], kbuf.at[s], ksem.at[s])

    def vcopy(l, c):
        s = slot_of(l, c)
        return pltpu.make_async_copy(v_hbm.at[l, pl.ds(c * CHUNK * 128, CHUNK * 128)], vbuf.at[s], vsem.at[s])

    def qcopy(l, i):
        r = pl.ds(i * 512, 512)
        return pltpu.make_async_copy(wqkv_hbm.at[l, r], wqkv.at[r], qsem.at[i])

    def ocopy(l, i):
        r = pl.ds(i * 256, 256)
        return pltpu.make_async_copy(wo_hbm.at[l, r], wo.at[r], osem.at[i])

    def gcopy(l, i):
        return pltpu.make_async_copy(wg_hbm.at[l, :, pl.ds(i * 512, 512)], wg.at[i], gsem.at[i])

    def ucopy(l, i):
        return pltpu.make_async_copy(wu_hbm.at[l, :, pl.ds(i * 512, 512)], wu.at[i], usem.at[i])

    def dcopy(l, i):
        return pltpu.make_async_copy(wd_hbm.at[l, :, pl.ds(i * CB, CB)], wd.at[i], dsem.at[i])

    def xcopy(i):
        return pltpu.make_async_copy(x_hbm.at[:, pl.ds(i * CB, CB)], xb.at[i], xsem.at[i])

    def ycopy(i, hf):
        rows = pl.ds(hf * HR, HR)
        return pltpu.make_async_copy(xb.at[i, rows], out_hbm.at[rows, pl.ds(i * CB, CB)], ysem.at[hf, i])

    def remote(src, dst, send, recv, dev):
        return pltpu.make_async_remote_copy(src_ref=src, dst_ref=dst, send_sem=send, recv_sem=recv,
                                            device_id={"tp": dev}, device_id_type=MESH)

    for i in range(NCB):
        xcopy(i).start()
    for i in range(4):
        qcopy(0, i).start()
    for c in range(LEAD[0]):
        kcopy(0, c).start()
        vcopy(0, c).start()
        if c == 0:
            for i in range(2):
                ocopy(0, i).start()

    lane = lax.broadcasted_iota(jnp.int32, (ROWS, 128), 1)
    first = lax.rem(lane, 64) < 32
    token = lax.shift_right_logical(lane, 3)

    pos = jnp.transpose(jnp.broadcast_to(lenv[...].astype(F32), (ROWS, 128)))
    ang = pos * inv[...]
    cs[...] = jnp.cos(ang)
    sn[...] = jnp.where(first, -jnp.sin(ang), jnp.sin(ang))

    def norm_rows(src, r0, g_ref, l):
        rows = pl.ds(r0, QR)
        ss = jnp.zeros((QR, CB), F32)
        for kb in range(NCB):
            v = src[kb, rows, :].astype(F32)
            ss = ss + v * v
        r = lax.rsqrt(jnp.sum(ss, axis=-1, keepdims=True) * (1.0 / D) + EPS)
        for kb in range(NCB):
            v = src[kb, rows, :].astype(F32)
            g = g_ref[l:l + 1, kb * CB:(kb + 1) * CB].astype(F32)
            an[rows, kb * CB:(kb + 1) * CB] = (v * r * g).astype(BF16)

    def project(l, r0, nr):
        rows = pl.ds(r0, nr)
        low = lane[:nr] < 64
        fst = first[:nr]

        def rope(t):
            other = jnp.where(fst, pltpu.roll(t, 96, 1), pltpu.roll(t, 32, 1))
            return (t * cs[rows, :] + other * sn[rows, :]).astype(BF16).astype(F32)

        for nb in range(3):
            z = _dot(an[rows, :], wqkv[:, nb * 256:(nb + 1) * 256]).astype(BF16).astype(F32)
            qkvs[2 * nb, rows, :] = z[:, :128]
            qkvs[2 * nb + 1, rows, :] = z[:, 128:]
        for j in range(2):
            for pr in range(2):
                t = rope(qkvs[3 * j + pr, rows, :])
                swapped = pltpu.roll(t, 64, 1)
                h = 4 * j + 2 * pr
                if j == 0:
                    even, odd = jnp.where(low, t, 0.0), jnp.where(low, swapped, 0.0)
                else:
                    even, odd = jnp.where(low, 0.0, swapped), jnp.where(low, 0.0, t)
                qs[pl.ds(r0 * HEADS + h, nr, stride=HEADS), :] = even
                qs[pl.ds(r0 * HEADS + h + 1, nr, stride=HEADS), :] = odd
        k0, k1 = rope(qkvs[2, rows, :]), rope(qkvs[5, rows, :])
        kn[rows, :] = jnp.where(low, k0, pltpu.roll(k1, 64, 1))
        vn[rows, :] = jnp.where(low, pltpu.roll(qkvs[2, rows, :], 64, 1), qkvs[5, rows, :])

    pos_s = lax.broadcasted_iota(jnp.int32, (8, SEQ), 1)

    def scores(l, c):
        s_ = slot_of(l, c)
        par, par4 = lax.rem(c, 2), lax.rem(c, 4)
        for t2 in range(CHUNK // 2):
            ps = []
            for t in (2 * t2, 2 * t2 + 1):
                b = c * CHUNK + t
                q = qs[pl.ds(b * 8, 8), :]
                new = jnp.sum(q * kn[pl.ds(b, 1), :], axis=-1, keepdims=True) * SCALE
                s = _dot(q.astype(BF16), kbuf[s_, t]) * SCALE
                s = jnp.where(pos_s < lens[b], s, -jnp.inf)
                m = jnp.maximum(jnp.max(s, axis=-1, keepdims=True), new)
                p = jnp.exp(s - m)
                pn = jnp.exp(new - m)
                den = jnp.sum(p, axis=-1, keepdims=True) + pn
                ps.append(p)
                stat[par4, 0, t * 8:(t + 1) * 8, :] = jnp.broadcast_to(pn, (8, 128))
                stat[par4, 1, t * 8:(t + 1) * 8, :] = jnp.broadcast_to(den, (8, 128))
            pbuf[par, t2 * 16:(t2 + 1) * 16, :] = jnp.concatenate(ps, axis=0).astype(BF16)

    def values(l, c):
        s_ = slot_of(l, c)
        par = lax.rem(c, 2)
        p = pbuf[par]
        acc = None
        for g in range(CHUNK // GV):
            res = lax.dot_general(vbuf[s_, g * GV * 128:(g + 1) * GV * 128, :], p, NT, preferred_element_type=F32)
            for t in range(GV):
                r = res[t * 128:(t + 1) * 128]
                acc = r if acc is None else jnp.where(token == g * GV + t, r, acc)
        accs[par] = acc

    def normalise(c, row):
        par, par4 = lax.rem(c, 2), lax.rem(c, 4)
        o = jnp.transpose(accs[par])
        v = jnp.concatenate([jnp.broadcast_to(vn[pl.ds(c * CHUNK + t, 1), :], (8, 128)) for t in range(CHUNK)], axis=0)
        os_[row:row + 128, :] = (o + stat[par4, 0] * v) / stat[par4, 1]

    low_q = lax.broadcasted_iota(jnp.int32, (QR, 128), 1) < 64

    def remote1o(q):
        rows = pl.ds(q * QR, QR)
        blocks = pl.ds((1 - core) * 4, 4)
        return remote(to.at[blocks, rows], r1o.at[:, rows], s1o.at[q], a1o.at[q], partner)

    def remote2o(q):
        rows = pl.ds(q * QR, QR)
        return remote(co.at[:, rows], r2o.at[:, rows], s2o.at[q], a2o.at[q], across)

    def remote3o(q):
        rows = pl.ds(q * QR, QR)
        blocks = pl.ds(core * 4, 4)
        return remote(hb.at[blocks, rows], hb.at[blocks, rows], s3o.at[q], a3o.at[q], partner)

    def out_proj(q):
        rows = pl.ds(q * QR, QR)
        normalise(2 * q, 0)
        normalise(2 * q + 1, 128)
        pairs = []
        for j in range(2):
            for pr in range(2):
                h = 4 * j + 2 * pr
                e = os_[pl.ds(h, QR, stride=HEADS), :]
                o = os_[pl.ds(h + 1, QR, stride=HEADS), :]
                if j == 0:
                    pairs.append(jnp.where(low_q, e, pltpu.roll(o, 64, 1)).astype(BF16))
                else:
                    pairs.append(jnp.where(low_q, pltpu.roll(e, 64, 1), o).astype(BF16))
        att = jnp.concatenate(pairs, axis=1)
        for nb in range(4):
            z = _dot(att, wo[:, nb * 512:(nb + 1) * 512]).astype(BF16)
            to[2 * nb, rows, :] = z[:, :CB]
            to[2 * nb + 1, rows, :] = z[:, CB:]
        remote1o(q).start()

    def chip_sum_o(q):
        rows = pl.ds(q * QR, QR)
        remote1o(q).wait_recv()
        for i in range(4):
            co[i, rows, :] = (to[core * 4 + i, rows, :].astype(F32) + r1o[i, rows, :].astype(F32)).astype(BF16)
        remote2o(q).start()

    def group_sum_o(q):
        rows = pl.ds(q * QR, QR)
        remote2o(q).wait_recv()
        for i in range(4):
            z = co[i, rows, :].astype(F32) + r2o[i, rows, :].astype(F32)
            hb[core * 4 + i, rows, :] = (xb[core * 4 + i, rows, :].astype(F32) + z).astype(BF16)
        remote3o(q).start()

    def finish_o(q, l):
        remote3o(q).wait_recv()
        norm_rows(hb, q * QR, g_mlp, l)

    def remote1m(hf, i):
        rows = pl.ds(hf * HR, HR)
        return remote(tm.at[(1 - core) * 4 + i, rows], r1m.at[i, rows], s1m.at[hf, i], a1m.at[hf, i], partner)

    def remote2m(hf, i):
        rows = pl.ds(hf * HR, HR)
        return remote(cm.at[i, rows], r2m.at[i, rows], s2m.at[hf, i], a2m.at[hf, i], across)

    def remote3m(hf, i):
        rows = pl.ds(hf * HR, HR)
        return remote(xb.at[core * 4 + i, rows], xb.at[core * 4 + i, rows], s3m.at[hf, i], a3m.at[hf, i], partner)

    def chip_sum_m(hf):
        rows = pl.ds(hf * HR, HR)
        for i in range(4):
            remote1m(hf, i).wait_recv()
            cm[i, rows, :] = (tm[core * 4 + i, rows, :].astype(F32) + r1m[i, rows, :].astype(F32)).astype(BF16)
            remote2m(hf, i).start()

    def group_sum_m(hf, last):
        rows = pl.ds(hf * HR, HR)
        for i in range(4):
            remote2m(hf, i).wait_recv()
            z = cm[i, rows, :].astype(F32) + r2m[i, rows, :].astype(F32)
            xb[core * 4 + i, rows, :] = (hb[core * 4 + i, rows, :].astype(F32) + z).astype(BF16)
            remote3m(hf, i).start()
            if last:
                ycopy(core * 4 + i, hf).start()

    def finish_m(hf, last):
        for i in range(4):
            remote3m(hf, i).wait_recv()
            if last:
                ycopy((1 - core) * 4 + i, hf).start()

    def drain_o():
        for q in range(NQ):
            remote1o(q).wait_send()
            remote2o(q).wait_send()
            remote3o(q).wait_send()

    def drain_m(hf):
        for i in range(4):
            remote1m(hf, i).wait_send()
            remote2m(hf, i).wait_send()
            remote3m(hf, i).wait_send()

    def mlp(l, hf, hooks):
        rows = pl.ds(hf * HR, HR)
        for n in range(4):
            if hf == 0:
                gcopy(l, n).wait()
                ucopy(l, n).wait()
            gate = _dot(an[rows, :], wg[n])
            up = _dot(an[rows, :], wu[n])
            act[rows, n * 512:(n + 1) * 512] = (jax.nn.silu(gate) * up).astype(BF16)
            for f in hooks.get(n, ()):
                f()
        for i in range(4):
            theirs, mine = (1 - core) * 4 + i, core * 4 + i
            if hf == 0:
                dcopy(l, theirs).wait()
                dcopy(l, mine).wait()
            tm[theirs, rows, :] = _dot(act[rows, :], wd[theirs]).astype(BF16)
            tm[mine, rows, :] = _dot(act[rows, :], wd[mine]).astype(BF16)
            remote1m(hf, i).start()
            for f in hooks.get(4 + i, ()):
                f()

    for i in range(NCB):
        xcopy(i).wait()

    for l in range(LAYERS):
        lead = LEAD[l]
        last = l + 1 == LAYERS

        def refill(i):
            @pl.when(i + lead < NCH)
            def _():
                kcopy(l, i + lead).start()

            @pl.when(jnp.logical_and(i >= 1, i - 1 + lead < NCH))
            def _():
                vcopy(l, i - 1 + lead).start()
            t = i + lead - NCH

            @pl.when(jnp.logical_and(t >= 0, t < 2))
            def _():
                for u in range(2):
                    gcopy(l, 2 * t + u).start()
                    ucopy(l, 2 * t + u).start()

            @pl.when(jnp.logical_and(t >= 2, t < 4))
            def _():
                for u in range(2):
                    dcopy(l, 2 * (t - 2) + u).start()
                    dcopy(l, 2 * (t - 2) + u + 4).start()

        def step(i):
            vcopy(l, i - 1).wait()
            kcopy(l, i).wait()
            scores(l, i)
            values(l, i - 1)
            refill(i)

        @pl.loop(0, NQ if l == 0 else NQ // 2)
        def _(q):
            norm_rows(xb, pl.multiple_of(q * QR, QR), g_attn, l)

        for i in range(4):
            qcopy(l, i).wait()
        project(l, 0, ROWS if l == 0 else HR)
        if l == 0:
            pl.semaphore_wait(barrier, 2)
        kcopy(l, 0).wait()
        scores(l, 0)
        refill(0)

        @pl.loop(1, 4)
        def _(i):
            step(i)

            @pl.when(i == 2)
            def _():
                for j in range(2):
                    ocopy(l, j).wait()
                out_proj(0)

            @pl.when(i == 3)
            def _():
                chip_sum_o(0)
            if l > 0:
                @pl.when(i == 1)
                def _():
                    group_sum_m(1, False)

        if l > 0:
            finish_m(1, False)
            drain_m(1)

            @pl.loop(NQ // 2, NQ)
            def _(q):
                norm_rows(xb, pl.multiple_of(q * QR, QR), g_attn, l)
            project(l, HR, HR)

        @pl.loop(4, NCH)
        def _(i):
            step(i)

            @pl.when(lax.rem(i, 2) == 0)
            def _():
                out_proj(i // 2 - 1)

            @pl.when(lax.rem(i, 2) == 1)
            def _():
                chip_sum_o((i - 3) // 2)

            @pl.when(i == 6)
            def _():
                group_sum_o(0)

        vcopy(l, NCH - 1).wait()
        values(l, NCH - 1)
        for t in range(max(0, lead), 4):
            for u in range(2):
                dcopy(l, 2 * (t - 2) + u).start()
                dcopy(l, 2 * (t - 2) + u + 4).start()
        if not last:
            for i in range(4):
                qcopy(l + 1, i).start()
        out_proj(3)
        group_sum_o(1)
        finish_o(0, l)
        finish_o(1, l)
        if not last:
            for i in range(2):
                ocopy(l + 1, i).start()
            for c in range(LEAD[l + 1]):
                kcopy(l + 1, c).start()
                vcopy(l + 1, c).start()
        mlp(l, 0, {0: (lambda: chip_sum_o(3),), 1: (lambda: group_sum_o(2),)})
        group_sum_o(3)
        finish_o(2, l)
        finish_o(3, l)
        mlp(l, 1, {0: (lambda: chip_sum_m(0),)})
        chip_sum_m(1)
        drain_o()
        group_sum_m(0, last)
        finish_m(0, last)
        drain_m(0)
        if last:
            group_sum_m(1, last)
            finish_m(1, last)
            drain_m(1)

    for i in range(NCB):
        for hf in range(2):
            ycopy(i, hf).wait()


def solution(mesh):
    half = HD // 2
    freq = np.float32(ROPE_THETA) ** (-np.arange(half, dtype=np.float32) * np.float32(2.0) / np.float32(HD))
    freq = np.tile(freq.astype(np.float32), 4)[None, :]

    def body(x, g_attn, w_qkv, w_o, g_mlp, w_gate, w_up, w_down, k_cache, v_cache, lengths):
        kt = jnp.transpose(k_cache, (0, 1, 3, 4, 2)).reshape(LAYERS, ROWS, 2 * HD, SEQ)
        vt = jnp.transpose(v_cache, (0, 1, 3, 4, 2)).reshape(LAYERS, ROWS * 2 * HD, SEQ)
        vm, hbm, sm = (pl.BlockSpec(memory_space=s) for s in (pltpu.VMEM, pl.ANY, pltpu.SMEM))
        V, DMA = pltpu.VMEM, pltpu.SemaphoreType.DMA
        scratch = [
            V((RING, CHUNK, 2 * HD, SEQ), BF16), V((RING, CHUNK * 2 * HD, SEQ), BF16),
            V((D, QKVL), BF16), V((512, D), BF16), V((4, D, 512), BF16), V((4, D, 512), BF16), V((NCB, FFL, CB), BF16),
            V((NCB, ROWS, CB), BF16), V((NCB, ROWS, CB), BF16), V((ROWS, D), BF16), V((ROWS, FFL), BF16),
            V((NCB, ROWS, CB), BF16), V((NCB, ROWS, CB), BF16),
            V((4, ROWS, CB), BF16), V((4, ROWS, CB), BF16), V((4, ROWS, CB), BF16), V((4, ROWS, CB), BF16),
            V((4, ROWS, CB), BF16), V((4, ROWS, CB), BF16),
            V((6, ROWS, 128), F32), V((ROWS * HEADS, 128), F32), V((256, 128), F32),
            V((ROWS, 128), F32), V((ROWS, 128), F32), V((ROWS, 128), F32), V((ROWS, 128), F32),
            V((2, 128, SEQ), BF16), V((4, 2, 128, 128), F32), V((2, 128, 128), F32),
            DMA((RING,)), DMA((RING,)), DMA((4,)), DMA((2,)), DMA((4,)), DMA((4,)), DMA((NCB,)), DMA((NCB,)),
            DMA((2, NCB)),
        ] + [DMA((4,)) for _ in range(6)] + [DMA((2, 4)) for _ in range(6)]
        return pl.pallas_call(
            _kernel,
            out_shape=jax.ShapeDtypeStruct((ROWS, D), BF16),
            in_specs=[sm, vm, vm, vm, vm] + [hbm] * 8,
            out_specs=hbm,
            scratch_shapes=scratch,
            compiler_params=pltpu.CompilerParams(collective_id=0, has_side_effects=True,
                                                 vmem_limit_bytes=67043328),
            name="decoder",
        )(lengths, lengths.reshape(1, ROWS), jnp.asarray(freq), g_attn, g_mlp, x, w_qkv, w_o, w_gate, w_up, w_down,
          kt, vt)

    col = P(None, None, 'tp')
    row = P(None, 'tp', None)
    cache = P(None, 'dp', None, 'tp', None)
    return jax.shard_map(body, mesh=mesh,
                         in_specs=(P('dp', None), P(), col, row, P(), col, col, row, cache, cache, P('dp')),
                         out_specs=P('dp', None), check_vma=False)
```

time: 80.7 us -> 72.3 us (0.90)
  Pallas kernels: 78.6 us -> 70 us
    pallas_call x1, Pallas kernels: 78.6 us -> 70 us  [body(): pl.pallas_call(_kernel, out_shape=jax.ShapeDtypeStruct((ROWS, D), BF16),...]
where the time goes in v2:
time: 72.3 us; the launch traced here: 71.9 us
  Pallas kernels  70 us (97%)
  local copies, waits for them, and re-layouts  1.88 us (3%)
    pallas_call x1, Pallas kernels, body(): pl.pallas_call(_kernel, out_shape=jax.ShapeDtypeStruct((ROWS, D), BF16),...  70 us
    unnamed x1, local copies, waits for them, and re-layouts  1.88 us

profile of v2, /device:TPU:0, one launch (start us, length us, event | category | flops | bytes accessed | tf_op | source)
XLA Modules:
  0.0 71.9 jit_solution(9720518793200624376)
XLA Ops:
  0.0 70.0 %decoder.1 = bf16[128,2048]{1,0:T(8,128)(2,1)} custom-call(s32[128]{0:T(128)} %lens.1, s32[1,128]{1,0:T(1,128)} %bitcast.9, f32[1,128]{1,0:T(1,128)} %constant.2.clone.inv, bf16[2,2048]{1,0:T(2,128)(2,1)} %g_attn.1, bf16[2,2048]{1,0:T(2,128)(2,1)} %g_mlp.1, bf16[128,2048]{1,0:T(8,128)(2,1)} %x_hbm.1, bf16[2,2048,768]{2,1,0:T(8,128)(2,1)} %wqkv_hbm.1, ...), custom_call_target="tpu_custom_call" | custom-call | tf_op jit(solution)/shard_map/decoder/pallas_call | solution.py:465
  70.0 1.9 %copy.14 = bf16[128,2048]{1,0:T(8,128)(2,1)} copy(bf16[128,2048]{1,0:T(8,128)(2,1)} %decoder.1) | data formatting | bytes 1048576

commit v3 on v2

--- a/solution.py
+++ b/solution.py
@@ -19,7 +19,6 @@
 CHUNK, NCH = 16, 8
 RING = 6
 LEAD = (3, RING)
-GV = 4
 QR, NQ = 32, 4
 HR = 64
 SCALE = HD ** -0.5
@@ -96,7 +95,6 @@
 
     lane = lax.broadcasted_iota(jnp.int32, (ROWS, 128), 1)
     first = lax.rem(lane, 64) < 32
-    token = lax.shift_right_logical(lane, 3)
 
     pos = jnp.transpose(jnp.broadcast_to(lenv[...].astype(F32), (ROWS, 128)))
     ang = pos * inv[...]
@@ -168,20 +166,15 @@
     def values(l, c):
         s_ = slot_of(l, c)
         par = lax.rem(c, 2)
-        p = pbuf[par]
-        acc = None
-        for g in range(CHUNK // GV):
-            res = lax.dot_general(vbuf[s_, g * GV * 128:(g + 1) * GV * 128, :], p, NT, preferred_element_type=F32)
-            for t in range(GV):
-                r = res[t * 128:(t + 1) * 128]
-                acc = r if acc is None else jnp.where(token == g * GV + t, r, acc)
-        accs[par] = acc
+        for t in range(CHUNK):
+            p = pbuf[par, t * 8:(t + 1) * 8, :]
+            accs[par, t * 8:(t + 1) * 8, :] = lax.dot_general(p, vbuf[s_, t * 128:(t + 1) * 128, :], NT,
+                                                              preferred_element_type=F32)
 
     def normalise(c, row):
         par, par4 = lax.rem(c, 2), lax.rem(c, 4)
-        o = jnp.transpose(accs[par])
         v = jnp.concatenate([jnp.broadcast_to(vn[pl.ds(c * CHUNK + t, 1), :], (8, 128)) for t in range(CHUNK)], axis=0)
-        os_[row:row + 128, :] = (o + stat[par4, 0] * v) / stat[par4, 1]
+        os_[row:row + 128, :] = (accs[par] + stat[par4, 0] * v) / stat[par4, 1]
 
     low_q = lax.broadcasted_iota(jnp.int32, (QR, 128), 1) < 64
 
@@ -286,27 +279,27 @@
             remote2m(hf, i).wait_send()
             remote3m(hf, i).wait_send()
 
-    def mlp(l, hf, hooks):
-        rows = pl.ds(hf * HR, HR)
-        for n in range(4):
+    def gate_up(l, hf, steps):
+        rows = pl.ds(hf * HR, HR)
+        for n in steps:
             if hf == 0:
                 gcopy(l, n).wait()
                 ucopy(l, n).wait()
+        for n in steps:
             gate = _dot(an[rows, :], wg[n])
             up = _dot(an[rows, :], wu[n])
             act[rows, n * 512:(n + 1) * 512] = (jax.nn.silu(gate) * up).astype(BF16)
-            for f in hooks.get(n, ()):
-                f()
+
+    def down(l, hf):
+        rows = pl.ds(hf * HR, HR)
+        if hf == 0:
+            for i in range(NCB):
+                dcopy(l, i).wait()
         for i in range(4):
             theirs, mine = (1 - core) * 4 + i, core * 4 + i
-            if hf == 0:
-                dcopy(l, theirs).wait()
-                dcopy(l, mine).wait()
             tm[theirs, rows, :] = _dot(act[rows, :], wd[theirs]).astype(BF16)
             tm[mine, rows, :] = _dot(act[rows, :], wd[mine]).astype(BF16)
             remote1m(hf, i).start()
-            for f in hooks.get(4 + i, ()):
-                f()
 
     for i in range(NCB):
         xcopy(i).wait()
@@ -419,11 +412,17 @@
             for c in range(LEAD[l + 1]):
                 kcopy(l + 1, c).start()
                 vcopy(l + 1, c).start()
-        mlp(l, 0, {0: (lambda: chip_sum_o(3),), 1: (lambda: group_sum_o(2),)})
+        gate_up(l, 0, (0,))
+        chip_sum_o(3)
+        gate_up(l, 0, (1, 2, 3))
+        group_sum_o(2)
+        down(l, 0)
         group_sum_o(3)
         finish_o(2, l)
         finish_o(3, l)
-        mlp(l, 1, {0: (lambda: chip_sum_m(0),)})
+        chip_sum_m(0)
+        gate_up(l, 1, range(4))
+        down(l, 1)
         chip_sum_m(1)
         drain_o()
         group_sum_m(0, last)

time: 72.3 us -> 69.7 us (0.964)
  Pallas kernels: 70 us -> 67.5 us
    pallas_call x1, Pallas kernels: 70 us -> 67.5 us  [body(): pl.pallas_call(_kernel, out_shape=jax.ShapeDtypeStruct((ROWS, D), BF16),...]
where the time goes in v3:
time: 69.7 us; the launch traced here: 69.4 us
  Pallas kernels  67.5 us (97%)
  local copies, waits for them, and re-layouts  1.88 us (3%)
    pallas_call x1, Pallas kernels, body(): pl.pallas_call(_kernel, out_shape=jax.ShapeDtypeStruct((ROWS, D), BF16),...  67.5 us
    unnamed x1, local copies, waits for them, and re-layouts  1.88 us

profile of v3, /device:TPU:0, one launch (start us, length us, event | category | flops | bytes accessed | tf_op | source)
XLA Modules:
  0.0 69.4 jit_solution(8820437642682388816)
XLA Ops:
  0.0 67.5 %decoder.1 = bf16[128,2048]{1,0:T(8,128)(2,1)} custom-call(s32[128]{0:T(128)} %lens.1, s32[1,128]{1,0:T(1,128)} %bitcast.9, f32[1,128]{1,0:T(1,128)} %constant.2.clone.inv, bf16[2,2048]{1,0:T(2,128)(2,1)} %g_attn.1, bf16[2,2048]{1,0:T(2,128)(2,1)} %g_mlp.1, bf16[128,2048]{1,0:T(8,128)(2,1)} %x_hbm.1, bf16[2,2048,768]{2,1,0:T(8,128)(2,1)} %wqkv_hbm.1, ...), custom_call_target="tpu_custom_call" | custom-call | tf_op jit(solution)/shard_map/decoder/pallas_call | solution.py:464
  67.5 1.9 %copy.14 = bf16[128,2048]{1,0:T(8,128)(2,1)} copy(bf16[128,2048]{1,0:T(8,128)(2,1)} %decoder.1) | data formatting | bytes 1048576

commit v4 on v3

--- a/solution.py
+++ b/solution.py
@@ -21,6 +21,7 @@
 LEAD = (3, RING)
 QR, NQ = 32, 4
 HR = 64
+VMEM_LIMIT = 64487424
 SCALE = HD ** -0.5
 NT = (((1,), (1,)), ((), ()))
 
@@ -30,10 +31,10 @@
 
 
 def _kernel(lens, lenv, inv, g_attn, g_mlp, x_hbm, wqkv_hbm, wo_hbm, wg_hbm, wu_hbm, wd_hbm, k_hbm, v_hbm,
-            out_hbm,
+            out_ref,
             kbuf, vbuf, wqkv, wo, wg, wu, wd, xb, hb, an, act, to, tm, r1o, r1m, co, cm, r2o, r2m,
             qkvs, qs, os_, kn, vn, cs, sn, pbuf, stat, accs,
-            ksem, vsem, qsem, osem, gsem, usem, dsem, xsem, ysem,
+            ksem, vsem, qsem, osem, gsem, usem, dsem, xsem,
             s1o, a1o, s2o, a2o, s3o, a3o, s1m, a1m, s2m, a2m, s3m, a3m):
     me = lax.axis_index("tp")
     core = lax.rem(me, 2)
@@ -73,10 +74,6 @@
 
     def xcopy(i):
         return pltpu.make_async_copy(x_hbm.at[:, pl.ds(i * CB, CB)], xb.at[i], xsem.at[i])
-
-    def ycopy(i, hf):
-        rows = pl.ds(hf * HR, HR)
-        return pltpu.make_async_copy(xb.at[i, rows], out_hbm.at[rows, pl.ds(i * CB, CB)], ysem.at[hf, i])
 
     def remote(src, dst, send, recv, dev):
         return pltpu.make_async_remote_copy(src_ref=src, dst_ref=dst, send_sem=send, recv_sem=recv,
@@ -244,28 +241,24 @@
         rows = pl.ds(hf * HR, HR)
         return remote(xb.at[core * 4 + i, rows], xb.at[core * 4 + i, rows], s3m.at[hf, i], a3m.at[hf, i], partner)
 
-    def chip_sum_m(hf):
-        rows = pl.ds(hf * HR, HR)
-        for i in range(4):
+    def chip_sum_m(hf, pieces):
+        rows = pl.ds(hf * HR, HR)
+        for i in pieces:
             remote1m(hf, i).wait_recv()
             cm[i, rows, :] = (tm[core * 4 + i, rows, :].astype(F32) + r1m[i, rows, :].astype(F32)).astype(BF16)
             remote2m(hf, i).start()
 
-    def group_sum_m(hf, last):
-        rows = pl.ds(hf * HR, HR)
-        for i in range(4):
+    def group_sum_m(hf, pieces):
+        rows = pl.ds(hf * HR, HR)
+        for i in pieces:
             remote2m(hf, i).wait_recv()
             z = cm[i, rows, :].astype(F32) + r2m[i, rows, :].astype(F32)
             xb[core * 4 + i, rows, :] = (hb[core * 4 + i, rows, :].astype(F32) + z).astype(BF16)
             remote3m(hf, i).start()
-            if last:
-                ycopy(core * 4 + i, hf).start()
-
-    def finish_m(hf, last):
+
+    def finish_m(hf):
         for i in range(4):
             remote3m(hf, i).wait_recv()
-            if last:
-                ycopy((1 - core) * 4 + i, hf).start()
 
     def drain_o():
         for q in range(NQ):
@@ -300,6 +293,9 @@
             tm[theirs, rows, :] = _dot(act[rows, :], wd[theirs]).astype(BF16)
             tm[mine, rows, :] = _dot(act[rows, :], wd[mine]).astype(BF16)
             remote1m(hf, i).start()
+            if i == 2:
+                chip_sum_m(hf, (0,))
+        chip_sum_m(hf, (1, 2, 3))
 
     for i in range(NCB):
         xcopy(i).wait()
@@ -308,34 +304,58 @@
         lead = LEAD[l]
         last = l + 1 == LAYERS
 
-        def refill(i):
-            @pl.when(i + lead < NCH)
-            def _():
-                kcopy(l, i + lead).start()
-
-            @pl.when(jnp.logical_and(i >= 1, i - 1 + lead < NCH))
-            def _():
-                vcopy(l, i - 1 + lead).start()
-            t = i + lead - NCH
-
-            @pl.when(jnp.logical_and(t >= 0, t < 2))
-            def _():
+        def when(cond, f):
+            if isinstance(cond, bool):
+                if cond:
+                    f()
+            else:
+                pl.when(cond)(f)
+
+        def refill_k(c):
+            when(c + lead < NCH, lambda: kcopy(l, c + lead).start())
+
+        def refill_v(c):
+            when(c + lead < NCH, lambda: vcopy(l, c + lead).start())
+
+        def refill_w(c):
+            t = c + lead - NCH
+
+            def gate_and_up():
                 for u in range(2):
                     gcopy(l, 2 * t + u).start()
                     ucopy(l, 2 * t + u).start()
 
-            @pl.when(jnp.logical_and(t >= 2, t < 4))
-            def _():
+            def down_pair():
                 for u in range(2):
                     dcopy(l, 2 * (t - 2) + u).start()
                     dcopy(l, 2 * (t - 2) + u + 4).start()
-
-        def step(i):
-            vcopy(l, i - 1).wait()
-            kcopy(l, i).wait()
-            scores(l, i)
-            values(l, i - 1)
-            refill(i)
+            if isinstance(t, int):
+                when(0 <= t < 2, gate_and_up)
+                when(2 <= t < 4, down_pair)
+            else:
+                when(jnp.logical_and(t >= 0, t < 2), gate_and_up)
+                when(jnp.logical_and(t >= 2, t < 4), down_pair)
+
+        def piece(k, ahead):
+            c = 2 * k
+            kcopy(l, c + 1).wait()
+            vcopy(l, c).wait()
+            vcopy(l, c + 1).wait()
+            if ahead:
+                kcopy(l, c + 2).wait()
+            scores(l, c + 1)
+            values(l, c)
+            if ahead:
+                scores(l, c + 2)
+            values(l, c + 1)
+            out_proj(k)
+            refill_k(c + 1)
+            refill_v(c)
+            refill_v(c + 1)
+            refill_w(c + 1)
+            if ahead:
+                refill_k(c + 2)
+                refill_w(c + 2)
 
         @pl.loop(0, NQ if l == 0 else NQ // 2)
         def _(q):
@@ -348,53 +368,57 @@
             pl.semaphore_wait(barrier, 2)
         kcopy(l, 0).wait()
         scores(l, 0)
-        refill(0)
-
-        @pl.loop(1, 4)
-        def _(i):
-            step(i)
-
-            @pl.when(i == 2)
-            def _():
-                for j in range(2):
-                    ocopy(l, j).wait()
-                out_proj(0)
-
-            @pl.when(i == 3)
-            def _():
-                chip_sum_o(0)
-            if l > 0:
-                @pl.when(i == 1)
+        refill_k(0)
+        refill_w(0)
+        for j in range(2):
+            ocopy(l, j).wait()
+        if l == 0:
+            @pl.loop(1, NCH)
+            def _(i):
+                vcopy(l, i - 1).wait()
+                kcopy(l, i).wait()
+                scores(l, i)
+                values(l, i - 1)
+                refill_k(i)
+                refill_v(i - 1)
+                refill_w(i)
+
+                @pl.when(jnp.logical_and(lax.rem(i, 2) == 0, i >= 2))
                 def _():
-                    group_sum_m(1, False)
-
-        if l > 0:
-            finish_m(1, False)
+                    out_proj(i // 2 - 1)
+
+                @pl.when(jnp.logical_and(lax.rem(i, 2) == 1, i >= 3))
+                def _():
+                    chip_sum_o((i - 3) // 2)
+
+                @pl.when(i == 6)
+                def _():
+                    group_sum_o(0)
+
+            vcopy(l, NCH - 1).wait()
+            values(l, NCH - 1)
+            out_proj(3)
+        else:
+            piece(0, True)
+            group_sum_m(1, range(4))
+            piece(1, False)
+            chip_sum_o(0)
+            finish_m(1)
             drain_m(1)
 
             @pl.loop(NQ // 2, NQ)
             def _(q):
                 norm_rows(xb, pl.multiple_of(q * QR, QR), g_attn, l)
             project(l, HR, HR)
-
-        @pl.loop(4, NCH)
-        def _(i):
-            step(i)
-
-            @pl.when(lax.rem(i, 2) == 0)
-            def _():
-                out_proj(i // 2 - 1)
-
-            @pl.when(lax.rem(i, 2) == 1)
-            def _():
-                chip_sum_o((i - 3) // 2)
-
-            @pl.when(i == 6)
-            def _():
-                group_sum_o(0)
-
-        vcopy(l, NCH - 1).wait()
-        values(l, NCH - 1)
+            kcopy(l, 4).wait()
+            scores(l, 4)
+            refill_k(4)
+            refill_w(4)
+            chip_sum_o(1)
+            piece(2, True)
+            group_sum_o(0)
+            piece(3, False)
+            chip_sum_o(2)
         for t in range(max(0, lead), 4):
             for u in range(2):
                 dcopy(l, 2 * (t - 2) + u).start()
@@ -402,7 +426,6 @@
         if not last:
             for i in range(4):
                 qcopy(l + 1, i).start()
-        out_proj(3)
         group_sum_o(1)
         finish_o(0, l)
         finish_o(1, l)
@@ -420,22 +443,20 @@
         group_sum_o(3)
         finish_o(2, l)
         finish_o(3, l)
-        chip_sum_m(0)
         gate_up(l, 1, range(4))
+        group_sum_m(0, (0,))
         down(l, 1)
-        chip_sum_m(1)
         drain_o()
-        group_sum_m(0, last)
-        finish_m(0, last)
+        group_sum_m(0, (1, 2, 3))
+        finish_m(0)
         drain_m(0)
         if last:
-            group_sum_m(1, last)
-            finish_m(1, last)
+            group_sum_m(1, range(4))
+            finish_m(1)
             drain_m(1)
 
     for i in range(NCB):
-        for hf in range(2):
-            ycopy(i, hf).wait()
+        out_ref[:, i * CB:(i + 1) * CB] = xb[i]
 
 
 def solution(mesh):
@@ -459,16 +480,15 @@
             V((ROWS, 128), F32), V((ROWS, 128), F32), V((ROWS, 128), F32), V((ROWS, 128), F32),
             V((2, 128, SEQ), BF16), V((4, 2, 128, 128), F32), V((2, 128, 128), F32),
             DMA((RING,)), DMA((RING,)), DMA((4,)), DMA((2,)), DMA((4,)), DMA((4,)), DMA((NCB,)), DMA((NCB,)),
-            DMA((2, NCB)),
         ] + [DMA((4,)) for _ in range(6)] + [DMA((2, 4)) for _ in range(6)]
         return pl.pallas_call(
             _kernel,
-            out_shape=jax.ShapeDtypeStruct((ROWS, D), BF16),
+            out_shape=pltpu.VMEM((ROWS, D), BF16),
             in_specs=[sm, vm, vm, vm, vm] + [hbm] * 8,
-            out_specs=hbm,
+            out_specs=vm,
             scratch_shapes=scratch,
             compiler_params=pltpu.CompilerParams(collective_id=0, has_side_effects=True,
-                                                 vmem_limit_bytes=67043328),
+                                                 vmem_limit_bytes=VMEM_LIMIT),
             name="decoder",
         )(lengths, lengths.reshape(1, ROWS), jnp.asarray(freq), g_attn, g_mlp, x, w_qkv, w_o, w_gate, w_up, w_down,
           kt, vt)

time: 69.7 us -> 69.6 us (level)
  Pallas kernels: 67.5 us -> 68.7 us
  local copies, waits for them, and re-layouts: 1.88 us -> 0.8 us
    pallas_call x1, Pallas kernels: 67.5 us -> 68.7 us  [body(): pl.pallas_call(_kernel, out_shape=pltpu.VMEM((ROWS, D), BF16), in_specs=[...]
    unnamed x1, local copies, waits for them, and re-layouts: 1.88 us -> 0.8 us
where the time goes in v4:
time: 69.6 us; the launch traced here: 69.5 us
  Pallas kernels  68.7 us (99%)
  local copies, waits for them, and re-layouts  0.8 us (1%)
    pallas_call x1, Pallas kernels, body(): pl.pallas_call(_kernel, out_shape=pltpu.VMEM((ROWS, D), BF16), in_specs=[...  68.7 us

profile of v4, /device:TPU:0, one launch (start us, length us, event | category | flops | bytes accessed | tf_op | source)
XLA Modules:
  0.0 69.5 jit_solution(5701004559271688759)
XLA Ops:
  0.0 68.7 %decoder.1 = bf16[128,2048]{1,0:T(8,128)(2,1)S(1)} custom-call(s32[128]{0:T(128)} %lens.1, s32[1,128]{1,0:T(1,128)} %bitcast.9, f32[1,128]{1,0:T(1,128)} %constant.2.clone.inv, bf16[2,2048]{1,0:T(2,128)(2,1)} %g_attn.1, bf16[2,2048]{1,0:T(2,128)(2,1)} %g_mlp.1, bf16[128,2048]{1,0:T(8,128)(2,1)} %x_hbm.1, bf16[2,2048,768]{2,1,0:T(8,128)(2,1)} %wqkv_hbm.1, ...), custom_call_target="tpu_custom_call" | custom-call | tf_op jit(solution)/shard_map/decoder/pallas_call | solution.py:484
  68.7 0.8 %copy.14 = bf16[128,2048]{1,0:T(8,128)(2,1)} copy(bf16[128,2048]{1,0:T(8,128)(2,1)S(1)} %decoder.1) | data formatting | bytes 1048576

commit v5 on v4

--- a/solution.py
+++ b/solution.py
@@ -292,10 +292,9 @@
             theirs, mine = (1 - core) * 4 + i, core * 4 + i
             tm[theirs, rows, :] = _dot(act[rows, :], wd[theirs]).astype(BF16)
             tm[mine, rows, :] = _dot(act[rows, :], wd[mine]).astype(BF16)
-            remote1m(hf, i).start()
-            if i == 2:
-                chip_sum_m(hf, (0,))
-        chip_sum_m(hf, (1, 2, 3))
+            if i % 2 == 1:
+                remote1m(hf, i - 1).start()
+                remote1m(hf, i).start()
 
     for i in range(NCB):
         xcopy(i).wait()
@@ -441,13 +440,14 @@
         group_sum_o(2)
         down(l, 0)
         group_sum_o(3)
+        chip_sum_m(0, range(4))
         finish_o(2, l)
         finish_o(3, l)
         gate_up(l, 1, range(4))
-        group_sum_m(0, (0,))
         down(l, 1)
         drain_o()
-        group_sum_m(0, (1, 2, 3))
+        group_sum_m(0, range(4))
+        chip_sum_m(1, range(4))
         finish_m(0)
         drain_m(0)
         if last:

time: 69.6 us -> 66.3 us (0.953)
  Pallas kernels: 68.7 us -> 65.3 us
    pallas_call x1, Pallas kernels: 68.7 us -> 65.3 us  [body(): pl.pallas_call(_kernel, out_shape=pltpu.VMEM((ROWS, D), BF16), in_specs=[...]
where the time goes in v5:
time: 66.3 us; the launch traced here: 66.1 us
  Pallas kernels  65.3 us (98%)
  local copies, waits for them, and re-layouts  0.8 us (1%)
    pallas_call x1, Pallas kernels, body(): pl.pallas_call(_kernel, out_shape=pltpu.VMEM((ROWS, D), BF16), in_specs=[...  65.3 us

profile of v5, /device:TPU:0, one launch (start us, length us, event | category | flops | bytes accessed | tf_op | source)
XLA Modules:
  0.0 66.1 jit_solution(8932450290723034713)
XLA Ops:
  0.0 65.3 %decoder.1 = bf16[128,2048]{1,0:T(8,128)(2,1)S(1)} custom-call(s32[128]{0:T(128)} %lens.1, s32[1,128]{1,0:T(1,128)} %bitcast.9, f32[1,128]{1,0:T(1,128)} %constant.2.clone.inv, bf16[2,2048]{1,0:T(2,128)(2,1)} %g_attn.1, bf16[2,2048]{1,0:T(2,128)(2,1)} %g_mlp.1, bf16[128,2048]{1,0:T(8,128)(2,1)} %x_hbm.1, bf16[2,2048,768]{2,1,0:T(8,128)(2,1)} %wqkv_hbm.1, ...), custom_call_target="tpu_custom_call" | custom-call | tf_op jit(solution)/shard_map/decoder/pallas_call | solution.py:484
  65.3 0.8 %copy.14 = bf16[128,2048]{1,0:T(8,128)(2,1)} copy(bf16[128,2048]{1,0:T(8,128)(2,1)S(1)} %decoder.1) | data formatting | bytes 1048576

commit v6 on v5

--- a/solution.py
+++ b/solution.py
@@ -292,9 +292,10 @@
             theirs, mine = (1 - core) * 4 + i, core * 4 + i
             tm[theirs, rows, :] = _dot(act[rows, :], wd[theirs]).astype(BF16)
             tm[mine, rows, :] = _dot(act[rows, :], wd[mine]).astype(BF16)
-            if i % 2 == 1:
-                remote1m(hf, i - 1).start()
-                remote1m(hf, i).start()
+            group = 2 if hf == 1 and l + 1 == LAYERS else 4
+            if (i + 1) % group == 0:
+                for u in range(i + 1 - group, i + 1):
+                    remote1m(hf, u).start()
 
     for i in range(NCB):
         xcopy(i).wait()

time: 66.3 us -> 66.2 us (level)
  no operation moved by 1% of the time
where the time goes in v6:
time: 66.2 us; the launch traced here: 66.1 us
  Pallas kernels  65.3 us (99%)
  local copies, waits for them, and re-layouts  0.8 us (1%)
    pallas_call x1, Pallas kernels, body(): pl.pallas_call(_kernel, out_shape=pltpu.VMEM((ROWS, D), BF16), in_specs=[...  65.3 us

profile of v6, /device:TPU:0, one launch (start us, length us, event | category | flops | bytes accessed | tf_op | source)
XLA Modules:
  0.0 66.1 jit_solution(16376013857828727098)
XLA Ops:
  0.0 65.3 %decoder.1 = bf16[128,2048]{1,0:T(8,128)(2,1)S(1)} custom-call(s32[128]{0:T(128)} %lens.1, s32[1,128]{1,0:T(1,128)} %bitcast.9, f32[1,128]{1,0:T(1,128)} %constant.2.clone.inv, bf16[2,2048]{1,0:T(2,128)(2,1)} %g_attn.1, bf16[2,2048]{1,0:T(2,128)(2,1)} %g_mlp.1, bf16[128,2048]{1,0:T(8,128)(2,1)} %x_hbm.1, bf16[2,2048,768]{2,1,0:T(8,128)(2,1)} %wqkv_hbm.1, ...), custom_call_target="tpu_custom_call" | custom-call | tf_op jit(solution)/shard_map/decoder/pallas_call | solution.py:485
  65.3 0.8 %copy.14 = bf16[128,2048]{1,0:T(8,128)(2,1)} copy(bf16[128,2048]{1,0:T(8,128)(2,1)S(1)} %decoder.1) | data formatting | bytes 1048576
